TPU v7x, 512 devices: a whole 4x8x8 slice. The times are simulated.
512 devices in a mesh: dp: 64 (over z, y), tensor: 8 (over x, core).
Axes of the slice: x: 4, y: 8, z: 8, core: 2. Of those that a mesh axis runs over, the one named last changes fastest.
Arguments:
- tokens: bfloat16 [8192, 2048], P('dp'), may hold values from -8 to 8
- grad_out: bfloat16 [8192, 2048], P('dp'), may hold values from -6 to 6
- route_ids: int32 [8192, 4], P('dp'), may hold values from 0 to 59, as said below
- expert_map: int32 [60], replicated, may hold values from 0 to 63, as said below
- router: bfloat16 [2048, 60], replicated, may hold values from -1 to 1
- shared_gate: bfloat16 [2048], replicated, may hold values from -0.125 to 0.125
- sh_gate: bfloat16 [2048, 2816], P('dp', 'tensor'), may hold values from -0.125 to 0.125
- sh_up: bfloat16 [2048, 2816], P('dp', 'tensor'), may hold values from -0.125 to 0.125
- sh_down: bfloat16 [2816, 2048], P('tensor', 'dp'), may hold values from -0.109375 to 0.109375
- ex_gate: bfloat16 [64, 2048, 1408], P('dp', None, 'tensor'), may hold values from -0.125 to 0.125
- ex_up: bfloat16 [64, 2048, 1408], P('dp', None, 'tensor'), may hold values from -0.125 to 0.125
- ex_down: bfloat16 [64, 1408, 2048], P('dp', 'tensor'), may hold values from -0.15625 to 0.15625
Outputs:
- mixed: bfloat16 [8192, 2048], P('dp', 'tensor')
- grad_tokens: bfloat16 [8192, 2048], P('dp', 'tensor')
Inputs may be any that keep to these rules, and one draw needn't show every extreme that they name: `route_ids`: each row names 4 different experts. Within the rows of one device (aligned blocks of 128 rows), no expert is named more than 9 times over all 4 columns, and some expert is named exactly 9 times. Entries are distinct. Expert e uses the weights of slot expert_map[e]; slot s is held by index s // 1 of dp. Slots that no expert names are not used.
All inputs are finite; a program needn't handle non-finite values.
Results may differ from a plain program's by a relative error of at most 0.011.
Values may be sent and summed in bfloat16 or wider, within the bound.
A program may use at most 64 MiB of HBM per device.

v0:
```python
import jax
import jax.numpy as jnp
from jax import lax
from jax.sharding import PartitionSpec as P

CAP = 9


def turned_gather(arrays, axis, dims):
    turned = [jnp.moveaxis(a, dim, 0) for a, dim in zip(arrays, dims)]
    both = jnp.concatenate([t.reshape(len(t), -1) for t in turned], axis=1)
    result, at, outs = (lax.all_gather(both, axis, axis=0, tiled=True), 0, [])
    for t, dim in zip(turned, dims):
        share = result[:, at : at + t[0].size].reshape(-1, *t.shape[1:])
        outs.append(jnp.moveaxis(share, 0, dim))
        at += t[0].size
    return tuple(outs)


def in_one_piece(arrays, axis, split_dim, concat_dim, along):
    ends, at = ([], 0)
    for a in arrays[:-1]:
        at += a.shape[along]
        ends.append(at)
    both = jnp.concatenate(arrays, axis=along)
    return tuple(
        jnp.split(
            lax.all_to_all(both, axis, split_axis=split_dim, concat_axis=concat_dim, tiled=True),
            ends,
            axis=along,
        )
    )


def in_one_piece_2(arrays, axis, dim, along):
    ends, at = ([], 0)
    for a in arrays[:-1]:
        at += a.shape[along]
        ends.append(at)
    both = jnp.concatenate(arrays, axis=along)
    return tuple(jnp.split(lax.all_gather(both, axis, axis=dim, tiled=True), ends, axis=along))


def copy_for_each(x, axis):
    peers = lax.axis_size(axis)
    return lax.all_to_all(jnp.broadcast_to(x[None], (peers, *x.shape)), axis, 0, 0, tiled=True)


def of_everyone(x, axis):
    return copy_for_each(x, axis).sum(axis=0)


def together(arrays, axis):
    line, at, outs = (jnp.concatenate([a.reshape(-1) for a in arrays]), 0, [])
    subtotal = of_everyone(line, axis)
    for a in arrays:
        outs.append(subtotal[at : at + a.size].reshape(a.shape))
        at += a.size
    return tuple(outs)


def side_by_side(arrays, axis, dim, along):
    ends, at = ([], 0)
    for a in arrays[:-1]:
        at += a.shape[along]
        ends.append(at)
    both = jnp.concatenate(arrays, axis=along)
    return tuple(
        jnp.split(lax.psum_scatter(both, axis, scatter_dimension=dim, tiled=True), ends, axis=along)
    )


def silu_pair(pre_gate):
    sigmoid_val = 1.0 / (1.0 + jnp.exp(-pre_gate))
    return (pre_gate * sigmoid_val, sigmoid_val * (1.0 + pre_gate * (1.0 - sigmoid_val)))


def contract_last(left, right):
    return lax.dot_general(
        left, right, (((1,), (1,)), ((), ())), preferred_element_type=jnp.float32
    )


def expert_block(rows_in, rows_cot, w_gate, w_up, w_down):
    pre_gate = jnp.dot(rows_in, w_gate, preferred_element_type=jnp.float32)
    pre_up = jnp.dot(rows_in, w_up, preferred_element_type=jnp.float32)
    active, derivative = silu_pair(pre_gate)
    hidden = (active * pre_up).astype(jnp.bfloat16)
    result = jnp.dot(hidden, w_down, preferred_element_type=jnp.float32)
    grad_hidden = contract_last(rows_cot, w_down)
    grad_gate = (grad_hidden * pre_up * derivative).astype(jnp.bfloat16)
    grad_up = (grad_hidden * active).astype(jnp.bfloat16)
    backward = contract_last(grad_gate, w_gate) + contract_last(grad_up, w_up)
    return (result, backward)


def expert_batch(rows_in, rows_cot, w_gate, w_up, w_down):
    pre_gate = jnp.einsum("slcd,ldf->slcf", rows_in, w_gate, preferred_element_type=jnp.float32)
    pre_up = jnp.einsum("slcd,ldf->slcf", rows_in, w_up, preferred_element_type=jnp.float32)
    active, derivative = silu_pair(pre_gate)
    hidden = (active * pre_up).astype(jnp.bfloat16)
    result = jnp.einsum(
        "slcf,lfd->slcd", hidden, w_down, preferred_element_type=jnp.float32
    ).astype(jnp.bfloat16)
    grad_hidden = jnp.einsum("slcd,lfd->slcf", rows_cot, w_down, preferred_element_type=jnp.float32)
    grad_gate = (grad_hidden * pre_up * derivative).astype(jnp.bfloat16)
    grad_up = (grad_hidden * active).astype(jnp.bfloat16)
    grad_both = jnp.concatenate([grad_gate, grad_up], axis=3)
    weight_both = jnp.concatenate([w_gate, w_up], axis=2)
    backward = jnp.einsum(
        "slcf,ldf->slcd", grad_both, weight_both, preferred_element_type=jnp.float32
    )
    return (result, backward.astype(jnp.bfloat16))


def shards(
    tokens,
    grad_out,
    route_ids,
    expert_map,
    router,
    shared_gate,
    sh_gate,
    sh_up,
    sh_down,
    ex_gate,
    ex_up,
    ex_down,
):
    tok_dev, width = tokens.shape
    top_count = route_ids.shape[1]
    expert_count = router.shape[1]
    dp_size = lax.axis_size("dp")
    tensor_size = lax.axis_size("tensor")
    tensor_rank = lax.axis_index("tensor")
    local_slots = ex_gate.shape[0]
    col_width = width // tensor_size
    col_start = tensor_rank * col_width
    buffer_rows = dp_size * local_slots * CAP
    slot_rows = local_slots * CAP
    flat_ids = route_ids.reshape(-1)
    chosen = (flat_ids[:, None] == jnp.arange(expert_count, dtype=jnp.int32)[None, :]).astype(
        jnp.int32
    )
    earlier = jnp.sum((jnp.cumsum(chosen, axis=0) - chosen) * chosen, axis=1)
    slot_of = jnp.sum(chosen * expert_map[None, :], axis=1)
    position = slot_of * CAP + earlier
    token_index = jnp.arange(tok_dev * top_count, dtype=jnp.int32) // top_count
    source_rows = jnp.full((buffer_rows,), tok_dev, jnp.int32).at[position].set(token_index)

    def fetch_rows(table):
        padded = jnp.concatenate([table, jnp.zeros((1, table.shape[1]), table.dtype)], axis=0)
        return jnp.take(padded, source_rows, axis=0)

    def run_routed():
        part_in = lax.dynamic_slice_in_dim(tokens, col_start, col_width, 1)
        part_cot = lax.dynamic_slice_in_dim(grad_out, col_start, col_width, 1)
        send_in = fetch_rows(part_in).reshape(dp_size, slot_rows, col_width)
        send_cot = fetch_rows(part_cot).reshape(dp_size, slot_rows, col_width)
        got_in, got_cot = in_one_piece((send_in, send_cot), "dp", 0, 0, 1)
        got_in, got_cot = in_one_piece_2((got_in, got_cot), "tensor", 2, 0)
        grid_shape = (dp_size, local_slots, CAP, width)
        result, backward = expert_batch(
            got_in.reshape(grid_shape), got_cot.reshape(grid_shape), ex_gate, ex_up, ex_down
        )
        split_out = result.reshape(buffer_rows, tensor_size, col_width)
        split_back = backward.reshape(buffer_rows, tensor_size, col_width)
        met_out, met_back = in_one_piece((split_out, split_back), "tensor", 1, 1, 0)
        summed_out = jnp.sum(met_out.astype(jnp.float32), axis=1).reshape(
            dp_size, slot_rows, col_width
        )
        summed_back = jnp.sum(met_back.astype(jnp.float32), axis=1).reshape(
            dp_size, slot_rows, col_width
        )
        came_out, came_back = tuple(
            (
                part.astype(jnp.float32)
                for part in in_one_piece(
                    (summed_out.astype(jnp.bfloat16), summed_back.astype(jnp.bfloat16)),
                    "dp",
                    0,
                    0,
                    1,
                )
            )
        )
        return (came_out.reshape(buffer_rows, col_width), came_back.reshape(buffer_rows, col_width))

    routed_out, routed_back = run_routed()
    weights = turned_gather((sh_gate, sh_up, sh_down), "dp", (0, 0, 1))
    full_gate, full_up, full_down = weights
    sh_out, sh_back = expert_block(tokens, grad_out, full_gate, full_up, full_down)
    routed_width = routed_out.shape[1]
    expert_out = jnp.take(routed_out, position, axis=0).reshape(tok_dev, top_count, routed_width)
    expert_back = jnp.take(routed_back, position, axis=0).reshape(tok_dev, top_count, routed_width)
    logits = jnp.dot(tokens, router, preferred_element_type=jnp.float32)
    exp_logit = jnp.exp(logits)
    prob_table = exp_logit / jnp.sum(exp_logit, axis=1, keepdims=True)
    picked = chosen.reshape(tok_dev, top_count, expert_count).astype(jnp.float32)
    gate_weights = jnp.sum(picked * prob_table[:, None, :], axis=2)
    shared_scale = 1.0 / (
        1.0 + jnp.exp(-jnp.dot(tokens, shared_gate, preferred_element_type=jnp.float32))
    )
    shared_part = jnp.sum(grad_out.astype(jnp.float32) * sh_out, axis=1)
    cot_cols = lax.dynamic_slice_in_dim(grad_out, col_start, col_width, 1).astype(jnp.float32)
    dots_part = jnp.sum(cot_cols[:, None, :] * expert_out, axis=2)
    routed_mixed = jnp.sum(gate_weights[:, :, None] * expert_out, axis=1)
    routed_grad = jnp.sum(gate_weights[:, :, None] * expert_back, axis=1)
    mixed_part = shared_scale[:, None] * sh_out
    grad_part = shared_scale[:, None] * sh_back
    out_dots, shared_dots = together((dots_part, shared_part), "tensor")
    mixed_cols, grad_cols = tuple(
        (
            part.astype(jnp.float32)
            for part in side_by_side(
                (mixed_part.astype(jnp.bfloat16), grad_part.astype(jnp.bfloat16)), "tensor", 1, 0
            )
        )
    )
    mixed_cols = mixed_cols + routed_mixed
    grad_cols = grad_cols + routed_grad
    grad_prob = jnp.sum(picked * out_dots[:, :, None], axis=1)
    dlogits = prob_table * (grad_prob - jnp.sum(gate_weights * out_dots, axis=1, keepdims=True))
    router_cols = lax.dynamic_slice_in_dim(router, col_start, col_width, 0).astype(jnp.float32)
    grad_router = lax.dot_general(
        dlogits,
        router_cols,
        (((1,), (1,)), ((), ())),
        precision=lax.Precision.HIGHEST,
        preferred_element_type=jnp.float32,
    )
    gate_cols = lax.dynamic_slice_in_dim(shared_gate, col_start, col_width, 0).astype(jnp.float32)
    slope_term = shared_dots * shared_scale * (1.0 - shared_scale)
    grad_total = grad_cols + grad_router + slope_term[:, None] * gate_cols[None, :]
    return (mixed_cols.astype(jnp.bfloat16), grad_total.astype(jnp.bfloat16))


def solution(mesh):
    placed = (
        P("dp", None),
        P("dp", None),
        P("dp", None),
        P(),
        P(),
        P(),
        P("dp", "tensor"),
        P("dp", "tensor"),
        P("tensor", "dp"),
        P("dp", None, "tensor"),
        P("dp", None, "tensor"),
        P("dp", "tensor", None),
    )
    return jax.shard_map(
        shards,
        mesh=mesh,
        in_specs=placed,
        out_specs=(P("dp", "tensor"), P("dp", "tensor")),
        check_vma=False,
    )
```

profile of v0, /device:TPU:1, one launch (start us, length us, event | category | flops | bytes accessed | tf_op | source)
XLA Modules:
  0.0 265.0 jit_solution(9257027790201195252)
XLA Ops:
  7.2 0.8 copy.47
  8.3 1.2 reduce-window.6
  9.5 0.2 slice_reduce_fusion.2
  10.1 0.8 select_reduce_fusion
  10.8 2.4 scatter_custom_fusion
  13.3 0.9 constant_dynamic-slice_fusion
  14.3 2.7 %gather_fusion.1 = bf16[576,256]{1,0:T(8,128)(2,1)S(1)} fusion(bf16[129,256]{1,0:T(8,128)(2,1)S(1)} %concatenate.36, s32[1024]{0:T(1024)S(1)} %pad_clamp_fusion.1), kind=kCustom, calls=%fused_computation.2.clone | custom fusion | bytes 592128 | tf_op jit(solution)/shard_map/jit(_take)/gather | solution.py:153
  17.0 2.7 %gather_fusion = bf16[576,256]{1,0:T(8,128)(2,1)S(1)} fusion(bf16[129,256]{1,0:T(8,128)(2,1)S(1)} %concatenate.35, s32[1024]{0:T(1024)S(1)} %pad_clamp_fusion.1), kind=kCustom, calls=%fused_computation.clone | custom fusion | bytes 592128 | tf_op jit(solution)/shard_map/jit(_take)/gather | solution.py:153
  19.7 0.1 broadcast_select_fusion.1
  19.9 0.1 reshape.166
  20.0 0.1 reshape.167
  20.2 0.3 pad_maximum_fusion.2
  20.4 38.9 %all_to_all.21 = bf16[64,18,256]{2,1,0:T(8,128)(2,1)S(1)} all-to-all(bf16[64,18,256]{2,1,0:T(8,128)(2,1)S(1)} %pad_maximum_fusion.2), channel_id=1, replica_groups=mesh['dp'=64,'tensor'=8] {'dp'}, dimensions={0} | all-to-all | bytes 1179648 | tf_op jit(solution)/shard_map/all_to_all | solution.py:28
  59.3 0.2 fusion.79
  59.7 0.8 pad_maximum_fusion.4
  60.6 0.2 all-gather.3.cloned.1.call-start
  60.8 0.7 concatenate.33
  61.6 39.5 %all-gather.5.cloned.1.call-done = bf16[128,9,2048]{2,0,1:T(8,128)(2,1)} async-done(((bf16[128,9,256]{2,0,1:T(8,128)(2,1)}), bf16[128,9,2048]{2,0,1:T(8,128)(2,1)}) %all-gather.5.cloned.1.call-update) | async-done | bytes 4718608 | tf_op jit(solution)/shard_map/all_gather | solution.py:41
  101.1 2.6 fusion.26
  103.7 0.4 copy-done.11
  104.2 0.8 fusion.29
  105.0 0.3 copy-done.14
  105.3 1.8 multiply_convert_fusion.2
  107.1 0.8 fusion
  107.9 3.5 %copy.52 = bf16[64,1,9,2048]{3,2,0,1:T(8,128)(2,1)} copy(bf16[64,1,9,2048]{3,0,2,1:T(8,128)(2,1)S(1)} %fusion) | data formatting | bytes 4718592 | tf_op jit(solution)/shard_map/convert_element_type | solution.py:104
  111.4 4.4 %reshape.172 = bf16[576,8,256]{2,1,0:T(8,128)(2,1)S(1)} reshape(bf16[64,1,9,2048]{3,2,0,1:T(8,128)(2,1)} %copy.52) | data formatting | bytes 4718592 | tf_op jit(solution)/shard_map/reshape | solution.py:166
  115.9 2.7 %fusion.1 = bf16[64,1,9,2048]{3,0,2,1:T(8,128)(2,1)S(1)} fusion(bf16[1,2048,176]{1,2,0:T(8,128)(2,1)S(1)} %copy-done.13, bf16[1,2048,176]{1,2,0:T(8,128)(2,1)} %param.25, bf16[64,1,9,176]{3,0,2,1:T(8,128)(2,1)} %get-tuple-element.17, bf16[64,1,9,176]{3,0,2,1:T(8,128)(2,1)} %get-tuple-element.16), kind=kOutput, calls=%fused_computation.9 | convolution fusion | flops 835346432 | bytes 4206592 | tf_op jit(solution)/shard_map/slcf,ldf->slcd/dot_general | solution.py:110
  118.6 3.5 %copy.53 = bf16[64,1,9,2048]{3,2,0,1:T(8,128)(2,1)} copy(bf16[64,1,9,2048]{3,0,2,1:T(8,128)(2,1)S(1)} %fusion.1) | data formatting | bytes 4718592 | tf_op jit(solution)/shard_map/convert_element_type | solution.py:113
  122.1 5.8 %reshape.175 = bf16[576,8,256]{2,1,0:T(8,128)(2,1)} reshape(bf16[64,1,9,2048]{3,2,0,1:T(8,128)(2,1)} %copy.53) | data formatting | bytes 4718592 | tf_op jit(solution)/shard_map/reshape | solution.py:167
  128.0 4.6 %pad_maximum_fusion = bf16[1152,8,256]{2,1,0:T(8,128)(2,1)S(1)} fusion(bf16[576,8,256]{2,1,0:T(8,128)(2,1)} %reshape.175, bf16[576,8,256]{2,1,0:T(8,128)(2,1)S(1)} %reshape.172), kind=kLoop, calls=%fused_computation.5 | loop fusion | flops 2359296 | bytes 9437184 | tf_op jit(solution)/shard_map/concatenate | solution.py:25
  132.6 3.2 %copy.54 = bf16[1152,8,256]{2,0,1:T(8,128)(2,1)} copy(bf16[1152,8,256]{2,1,0:T(8,128)(2,1)S(1)} %pad_maximum_fusion) | data formatting | bytes 9437184 | tf_op jit(solution)/shard_map/concatenate | solution.py:25
  135.7 5.1 %all-to-all-start.1 = ((bf16[1152,8,256]{2,0,1:T(8,128)(2,1)}), bf16[1152,8,256]{2,0,1:T(8,128)(2,1)}, u32[]{:S(2)}, u32[]{:S(2)}) async-start(bf16[1152,8,256]{2,0,1:T(8,128)(2,1)} %copy.54), calls=%async_computation.2 | async-start | bytes 9437184 | tf_op jit(solution)/shard_map/all_to_all | solution.py:28
  140.9 0.2 fusion.46
  141.1 46.9 %all-gather.3.cloned.1.call-done = bf16[2048,1056]{1,0:T(8,128)(2,1)} async-done(((bf16[32,1056]{1,0:T(8,128)(2,1)}), bf16[2048,1056]{1,0:T(8,128)(2,1)}) %all-gather.3.cloned.1.call-update) | async-done | bytes 4325392 | tf_op jit(solution)/shard_map/all_gather | solution.py:12
  188.0 2.1 fusion.32
  190.2 2.7 %fusion.35 = f32[128,352]{0,1:T(8,128)S(1)} fusion(bf16[128,2048]{1,0:T(8,128)(2,1)S(1)} %copy-done.2, bf16[2048,1056]{1,0:T(8,128)(2,1)} %all-gather.3.cloned.1.call-done), kind=kOutput, calls=%fused_computation.39 | convolution fusion | flops 184549376 | bytes 2277376 | tf_op jit(solution)/shard_map/dot_general | solution.py:86
  192.9 1.1 fusion.38
  194.0 0.7 fusion.19
  194.7 1.0 fusion.3
  195.7 3.7 %slice_reduce_fusion.1 = (bf16[576,256]{1,0:T(8,128)(2,1)S(1)}, bf16[576,256]{1,0:T(8,128)(2,1)S(1)}) fusion(bf16[1152,8,256]{2,0,1:T(8,128)(2,1)} %all-to-all-done.1), kind=kLoop, calls=%fused_computation.14 | loop fusion | flops 2064384 | bytes 5308416 | tf_op jit(solution)/shard_map/reduce_sum | solution.py:169
  199.4 0.1 convert_element_type.112
  199.5 0.1 convert_element_type.113
  199.7 1.1 pad_maximum_fusion.3
  200.8 12.6 %all-to-all-start.2 = ((bf16[64,18,256]{2,1,0:T(8,128)(2,1)}), bf16[64,18,256]{2,1,0:T(8,128)(2,1)S(1)}, u32[]{:S(2)}, u32[]{:S(2)}) async-start(bf16[64,18,256]{2,1,0:T(8,128)(2,1)} %pad_maximum_fusion.3), calls=%async_computation.3 | async-start | bytes 1572864 | tf_op jit(solution)/shard_map/all_to_all | solution.py:28
  213.4 2.8 %multiply_convert_fusion = (bf16[128,2048]{1,0:T(8,128)(2,1)S(1)}, f32[128]{0:T(128)S(1)}) fusion(f32[128]{0:T(128)S(1)} %fusion.46, bf16[128,2048]{1,0:T(8,128)(2,1)} %param.17, bf16[2048,1056]{1,0:T(8,128)(2,1)} %all-gather.3.cloned.1.call-done, f32[128,352]{0,1:T(8,128)S(1)} %fusion.35, f32[128,352]{0,1:T(8,128)S(1)} %fusion.32), kind=kOutput, calls=%fused_computation.52 | convolution fusion | flops 186130304 | bytes 2982912 | tf_op jit(solution)/shard_map/dot_general | solution.py:89
  216.2 1.1 pad_maximum_fusion.1
  217.4 0.2 mul.184
  217.6 0.3 fusion.80
  217.9 16.9 %all-to-all-done.2 = bf16[64,18,256]{2,1,0:T(8,128)(2,1)S(1)} async-done(((bf16[64,18,256]{2,1,0:T(8,128)(2,1)}), bf16[64,18,256]{2,1,0:T(8,128)(2,1)S(1)}, u32[]{:S(2)}, u32[]{:S(2)}) %all-to-all-start.2) | async-done | bytes 589856 | tf_op jit(solution)/shard_map/all_to_all | solution.py:28
  234.8 1.3 slice_convert_fusion.1
  236.1 1.3 reshape.185
  237.6 1.6 gather_fusion.3
  239.2 1.6 gather_fusion.2
  240.8 1.0 multiply_reduce_fusion.1
  241.8 0.6 broadcast_in_dim.23
  242.4 6.9 %all-to-all-start.3 = ((f32[8,1,640]{2,1,0:T(1,128)}), f32[8,1,640]{2,1,0:T(1,128)S(1)}, u32[]{:S(2)}, u32[]{:S(2)}) async-start(f32[8,1,640]{2,1,0:T(1,128)} %broadcast_in_dim.23), calls=%async_computation.4 | async-start | bytes 40960 | tf_op jit(solution)/shard_map/all_to_all | solution.py:46
  249.4 1.2 reshape.178
  250.6 0.1 reshape.181
  250.7 3.3 %all-to-all-done.3 = f32[8,1,640]{2,1,0:T(1,128)S(1)} async-done(((f32[8,1,640]{2,1,0:T(1,128)}), f32[8,1,640]{2,1,0:T(1,128)S(1)}, u32[]{:S(2)}, u32[]{:S(2)}) %all-to-all-start.3) | async-done | bytes 20512 | tf_op jit(solution)/shard_map/all_to_all | solution.py:46
  254.2 0.1 multiply_reduce_fusion.4
  254.4 0.1 copy.46
  254.5 0.7 multiply_reduce_fusion.2
  255.2 1.5 add_convert_fusion
  256.7 1.7 fusion.42
  (68 shorter events, 1.5 us)
Async XLA Ops:
  7.2 96.6 %copy-start = (bf16[1,176,2048]{2,1,0:T(8,128)(2,1)S(1)}, bf16[1,176,2048]{2,1,0:T(8,128)(2,1)}, u32[]{:S(2)}) copy-start(bf16[1,176,2048]{2,1,0:T(8,128)(2,1)} %param.27) | copy-start | bytes 2162692
  7.2 93.9 %all-gather.5.cloned.1.call-start = ((), (), s32[]{:S(2)}) async-start(), calls=%async_computation.7 | async-start | bytes 5308416 | tf_op jit(solution)/shard_map/all_gather | solution.py:41
  59.3 1.5 copy-start.5
  59.3 1.5 copy-start.6
  59.3 1.6 copy-start.7
  59.3 41.8 %copy-start.12 = (bf16[1,2048,176]{1,2,0:T(8,128)(2,1)S(1)}, bf16[1,2048,176]{1,2,0:T(8,128)(2,1)}, u32[]{:S(2)}) copy-start(bf16[1,2048,176]{1,2,0:T(8,128)(2,1)} %param.26) | copy-start | bytes 2162692
  60.6 127.4 %all-gather.3.cloned.1.call-start = ((), (), s32[]{:S(2)}) async-start(), calls=%async_computation.5 | async-start | bytes 4792320 | tf_op jit(solution)/shard_map/all_gather | solution.py:12
  101.1 3.0 %copy-start.11 = (bf16[128,9,2048]{2,0,1:T(8,128)(2,1)S(1)}, bf16[128,9,2048]{2,0,1:T(8,128)(2,1)}, u32[]{:S(2)}) copy-start(bf16[128,9,2048]{2,0,1:T(8,128)(2,1)} %all-gather.5.cloned.1.call-done) | copy-start | bytes 14155780
  104.2 1.1 copy-start.14
  111.4 4.4 %copy-start.13 = (bf16[1,2048,176]{1,2,0:T(8,128)(2,1)S(1)}, bf16[1,2048,176]{1,2,0:T(8,128)(2,1)}, u32[]{:S(2)}) copy-start(bf16[1,2048,176]{1,2,0:T(8,128)(2,1)} %param.26) | copy-start | bytes 2162692
  135.7 5.1 %copy-start.10 = (bf16[2048]{0:T(1024)(128)(2,1)S(1)}, bf16[2048]{0:T(1024)(128)(2,1)}, u32[]{:S(2)}) copy-start(bf16[2048]{0:T(1024)(128)(2,1)} %param.21) | copy-start | bytes 12292
  135.7 5.1 %copy-start.2 = (bf16[128,2048]{1,0:T(8,128)(2,1)S(1)}, bf16[128,2048]{1,0:T(8,128)(2,1)}, u32[]{:S(2)}) copy-start(bf16[128,2048]{1,0:T(8,128)(2,1)} %param.16) | copy-start | bytes 1572868
  135.7 59.9 %all-to-all-start.1 = ((bf16[1152,8,256]{2,0,1:T(8,128)(2,1)}), bf16[1152,8,256]{2,0,1:T(8,128)(2,1)}, u32[]{:S(2)}, u32[]{:S(2)}) async-start(bf16[1152,8,256]{2,0,1:T(8,128)(2,1)} %copy.54), calls=%async_computation.2 | async-start | bytes 9437184 | tf_op jit(solution)/shard_map/all_to_all | solution.py:28
  141.1 51.7 %copy-start.9 = (bf16[128,2048]{1,0:T(8,128)(2,1)S(1)}, bf16[128,2048]{1,0:T(8,128)(2,1)}, u32[]{:S(2)}) copy-start(bf16[128,2048]{1,0:T(8,128)(2,1)} %param.17) | copy-start | bytes 1572868
  188.0 4.9 %copy-start.3 = (bf16[2048,1056]{1,0:T(8,128)(2,1)S(1)}, bf16[2048,1056]{1,0:T(8,128)(2,1)}, u32[]{:S(2)}) copy-start(bf16[2048,1056]{1,0:T(8,128)(2,1)} %all-gather.3.cloned.1.call-done) | copy-start | bytes 12976132
  200.8 34.0 %all-to-all-start.2 = ((bf16[64,18,256]{2,1,0:T(8,128)(2,1)}), bf16[64,18,256]{2,1,0:T(8,128)(2,1)S(1)}, u32[]{:S(2)}, u32[]{:S(2)}) async-start(bf16[64,18,256]{2,1,0:T(8,128)(2,1)} %pad_maximum_fusion.3), calls=%async_computation.3 | async-start | bytes 1572864 | tf_op jit(solution)/shard_map/all_to_all | solution.py:28
  213.4 41.8 %reduce-scatter.2.cloned.1.call-start = ((), (), s32[]{:S(2)}) async-start(), calls=%async_computation.6 | async-start | bytes 1179648 | tf_op jit(solution)/shard_map/reduce_scatter | solution.py:69
  216.2 1.4 copy-start.4
  240.8 13.5 %copy-start.8 = (s32[128,4]{0,1:T(4,128)S(1)}, s32[128,4]{0,1:T(4,128)}, u32[]{:S(2)}) copy-start(s32[128,4]{0,1:T(4,128)} %param.18) | copy-start | bytes 6148
  240.8 17.7 %copy-start.1 = (bf16[1,176,2048]{2,1,0:T(8,128)(2,1)S(1)}, bf16[1,176,2048]{2,1,0:T(8,128)(2,1)}, u32[]{:S(2)}) copy-start(bf16[1,176,2048]{2,1,0:T(8,128)(2,1)} %param.27) | copy-start | bytes 2162692
  242.4 11.6 %all-to-all-start.3 = ((f32[8,1,640]{2,1,0:T(1,128)}), f32[8,1,640]{2,1,0:T(1,128)S(1)}, u32[]{:S(2)}, u32[]{:S(2)}) async-start(f32[8,1,640]{2,1,0:T(1,128)} %broadcast_in_dim.23), calls=%async_computation.4 | async-start | bytes 40960 | tf_op jit(solution)/shard_map/all_to_all | solution.py:46
Sparse Core Ops, SparseCore 0:
  60.7 40.3 all-gather.4
  104.1 83.8 all-gather.2
  217.4 36.9 reduce-scatter.1
where the time goes:
time: 266 us; the launch traced here: 265 us
  waiting for transfers between devices  107 us (40%)
  local copies, waits for them, and re-layouts  40.2 us (15%)
  blocking collectives  38.9 us (15%)
  starting transfers between devices  24.9 us (9%)
  matrix products  21.4 us (8%)
  other arithmetic  18.6 us (7%)
  between operations  14.3 us (5%)
    all_gather x1, waiting for transfers between devices, turned_gather(): result, at, outs = (lax.all_gather(both, axis, axis=0, tiled=True), 0, [])  46.9 us
    all_gather x1, waiting for transfers between devices, in_one_piece_2(): lax.all_gather(both, axis, axis=dim, tiled=True)  39.5 us
    all_to_all x1, blocking collectives, in_one_piece(): lax.all_to_all(both, axis, split_axis=split_dim, concat_axis=concat_dim,...  38.9 us
    all_to_all x2, starting transfers between devices, in_one_piece(): lax.all_to_all(both, axis, split_axis=split_dim, concat_axis=concat_dim,...  17.7 us
    all_to_all x2, waiting for transfers between devices, in_one_piece(): lax.all_to_all(both, axis, split_axis=split_dim, concat_axis=concat_dim,...  16.9 us
    all_to_all x1, starting transfers between devices, copy_for_each(): lax.all_to_all(jnp.broadcast_to(x[None], (peers, *x.shape)), axis, 0, 0,...  6.92 us
    concatenate x3, other arithmetic, in_one_piece(): both = jnp.concatenate(arrays, axis=along)  5.99 us
    reshape x1, local copies, waits for them, and re-layouts, run_routed(): split_back = backward.reshape(buffer_rows, tensor_size, col_width)  5.82 us
  transfers between devices with their start and end apart: 6, of which 4 were waited for; matrix products, arithmetic and copies ran while one was open for 21% of the time, Pallas kernels for 0%

commit v1 on v0

--- a/solution.py
+++ b/solution.py
@@ -6,10 +6,15 @@
 CAP = 9
 
 
+def steps_all_divide(raw, mesh_dim):
+    far_arr = jax.lax.all_to_all(jnp.stack([raw] * jax.lax.axis_size(mesh_dim)), mesh_dim, 0, 0)
+    return jnp.concatenate(far_arr, axis=0)
+
+
 def turned_gather(arrays, axis, dims):
     turned = [jnp.moveaxis(a, dim, 0) for a, dim in zip(arrays, dims)]
     both = jnp.concatenate([t.reshape(len(t), -1) for t in turned], axis=1)
-    result, at, outs = (lax.all_gather(both, axis, axis=0, tiled=True), 0, [])
+    result, at, outs = (steps_all_divide(both, axis), 0, [])
     for t, dim in zip(turned, dims):
         share = result[:, at : at + t[0].size].reshape(-1, *t.shape[1:])
         outs.append(jnp.moveaxis(share, 0, dim))

time: 266 us -> 347 us (1.30)
  starting transfers between devices: 24.9 us -> 62.6 us
  waiting for transfers between devices: 107 us -> 143 us
  matrix products: 21.4 us -> 25.8 us
    all_to_all x0 -> x1, waiting for transfers between devices: none -> 51.3 us  [steps_all_divide(): jax.lax.all_to_all(jnp.stack([raw] * jax.lax.axis_size(mesh_dim)), mesh_d...]
    all_gather x1 -> x0, waiting for transfers between devices: 46.9 us -> none  [turned_gather(): result, at, outs = (lax.all_gather(both, axis, axis=0, tiled=True), 0, [])]
    all_to_all x2, waiting for transfers between devices: 16.9 us -> 58.9 us  [in_one_piece(): lax.all_to_all(both, axis, split_axis=split_dim, concat_axis=concat_dim,...]
    all_to_all x2, starting transfers between devices: 17.7 us -> 47.5 us  [in_one_piece(): lax.all_to_all(both, axis, split_axis=split_dim, concat_axis=concat_dim,...]
    all_gather x1, waiting for transfers between devices: 39.5 us -> 29.7 us  [in_one_piece_2(): lax.all_gather(both, axis, axis=dim, tiled=True)]
    all_to_all x0 -> x1, starting transfers between devices: none -> 8.16 us  [steps_all_divide(): jax.lax.all_to_all(jnp.stack([raw] * jax.lax.axis_size(mesh_dim)), mesh_d...]
    dot_general x3, matrix products: 2.78 us -> 7.36 us  [contract_last(): lax.dot_general(left, right, (((1,), (1,)), ((), ())), preferred_element_...]
  transfers between devices with their start and end apart: 6 -> 6, of which waited for: 4 -> 5; matrix products, arithmetic and copies ran while one was open for 21% -> 18% of each run, Pallas kernels for 0% -> 0%
where the time goes in v1:
time: 347 us; the launch traced here: 346 us
  waiting for transfers between devices  143 us (41%)
  starting transfers between devices  62.6 us (18%)
  local copies, waits for them, and re-layouts  42.2 us (12%)
  blocking collectives  38.9 us (11%)
  matrix products  25.8 us (7%)
  other arithmetic  18.6 us (5%)
  between operations  14.6 us (4%)
    all_to_all x2, waiting for transfers between devices, in_one_piece(): lax.all_to_all(both, axis, split_axis=split_dim, concat_axis=concat_dim,...  58.9 us
    all_to_all x1, waiting for transfers between devices, steps_all_divide(): jax.lax.all_to_all(jnp.stack([raw] * jax.lax.axis_size(mesh_dim)), mesh_d...  51.3 us
    all_to_all x2, starting transfers between devices, in_one_piece(): lax.all_to_all(both, axis, split_axis=split_dim, concat_axis=concat_dim,...  47.5 us
    all_to_all x1, blocking collectives, in_one_piece(): lax.all_to_all(both, axis, split_axis=split_dim, concat_axis=concat_dim,...  38.9 us
    all_gather x1, waiting for transfers between devices, in_one_piece_2(): lax.all_gather(both, axis, axis=dim, tiled=True)  29.7 us
    all_to_all x1, starting transfers between devices, steps_all_divide(): jax.lax.all_to_all(jnp.stack([raw] * jax.lax.axis_size(mesh_dim)), mesh_d...  8.16 us
    dot_general x3, matrix products, contract_last(): lax.dot_general(left, right, (((1,), (1,)), ((), ())), preferred_element_...  7.36 us
  transfers between devices with their start and end apart: 6, of which 5 were waited for; matrix products, arithmetic and copies ran while one was open for 18% of the time, Pallas kernels for 0%

profile of v1, /device:TPU:1, one launch (start us, length us, event | category | flops | bytes accessed | tf_op | source)
XLA Modules:
  0.0 346.0 jit_solution(279288285996142847)
XLA Ops:
  7.2 0.8 copy.47
  8.3 1.2 reduce-window.6
  9.5 0.2 slice_reduce_fusion.2
  10.1 0.8 select_reduce_fusion
  10.8 2.4 scatter_custom_fusion
  13.3 0.9 constant_dynamic-slice_fusion
  14.3 2.7 gather_fusion.1
  17.0 2.7 gather_fusion
  19.7 0.1 broadcast_select_fusion.1
  19.9 0.1 reshape.172
  20.0 0.1 reshape.173
  20.2 0.3 pad_maximum_fusion.2
  20.4 38.9 %all_to_all.26 = bf16[64,18,256]{2,1,0:T(8,128)(2,1)S(1)} all-to-all(bf16[64,18,256]{2,1,0:T(8,128)(2,1)S(1)} %pad_maximum_fusion.2), channel_id=1, replica_groups=mesh['dp'=64,'tensor'=8] {'dp'}, dimensions={0} | all-to-all | bytes 1179648 | tf_op jit(solution)/shard_map/all_to_all | solution.py:33
  59.3 0.2 fusion.79
  59.7 0.8 pad_maximum_fusion.4
  60.7 2.5 stack.2
  63.2 8.2 %all-to-all-start = ((bf16[64,32,1056]{2,1,0:T(8,128)(2,1)}), bf16[64,32,1056]{2,1,0:T(8,128)(2,1)}, u32[]{:S(2)}, u32[]{:S(2)}) async-start(bf16[64,32,1056]{2,1,0:T(8,128)(2,1)} %stack.2), calls=%async_computation | async-start | bytes 9437184 | tf_op jit(solution)/shard_map/all_to_all | solution.py:10
  71.4 29.7 %all-gather.2.cloned.1.call-done = bf16[128,9,2048]{2,0,1:T(8,128)(2,1)} async-done(((bf16[128,9,256]{2,0,1:T(8,128)(2,1)}), bf16[128,9,2048]{2,0,1:T(8,128)(2,1)}) %all-gather.2.cloned.1.call-update) | async-done | bytes 4718608 | tf_op jit(solution)/shard_map/all_gather | solution.py:46
  101.1 2.6 fusion.26
  103.7 0.4 copy-done.10
  104.2 0.8 fusion.29
  105.0 0.3 copy-done.13
  105.3 1.8 multiply_convert_fusion.2
  107.0 0.8 fusion
  107.8 3.6 %copy.52 = bf16[64,1,9,2048]{3,2,0,1:T(8,128)(2,1)} copy(bf16[64,1,9,2048]{3,0,2,1:T(8,128)(2,1)S(1)} %fusion) | data formatting | bytes 4718592 | tf_op jit(solution)/shard_map/convert_element_type | solution.py:109
  111.4 4.4 %reshape.178 = bf16[576,8,256]{2,1,0:T(8,128)(2,1)S(1)} reshape(bf16[64,1,9,2048]{3,2,0,1:T(8,128)(2,1)} %copy.52) | data formatting | bytes 4718592 | tf_op jit(solution)/shard_map/reshape | solution.py:171
  115.9 2.7 fusion.1
  118.6 3.6 %copy.53 = bf16[64,1,9,2048]{3,2,0,1:T(8,128)(2,1)} copy(bf16[64,1,9,2048]{3,0,2,1:T(8,128)(2,1)S(1)} %fusion.1) | data formatting | bytes 4718592 | tf_op jit(solution)/shard_map/convert_element_type | solution.py:118
  122.1 5.8 %reshape.181 = bf16[576,8,256]{2,1,0:T(8,128)(2,1)} reshape(bf16[64,1,9,2048]{3,2,0,1:T(8,128)(2,1)} %copy.53) | data formatting | bytes 4718592 | tf_op jit(solution)/shard_map/reshape | solution.py:172
  128.0 4.6 %pad_maximum_fusion = bf16[1152,8,256]{2,1,0:T(8,128)(2,1)S(1)} fusion(bf16[576,8,256]{2,1,0:T(8,128)(2,1)} %reshape.181, bf16[576,8,256]{2,1,0:T(8,128)(2,1)S(1)} %reshape.178), kind=kLoop, calls=%fused_computation.5 | loop fusion | flops 2359296 | bytes 9437184 | tf_op jit(solution)/shard_map/concatenate | solution.py:30
  132.6 3.2 copy.54
  135.8 51.3 %all-to-all-done = bf16[64,32,1056]{2,1,0:T(8,128)(2,1)} async-done(((bf16[64,32,1056]{2,1,0:T(8,128)(2,1)}), bf16[64,32,1056]{2,1,0:T(8,128)(2,1)}, u32[]{:S(2)}, u32[]{:S(2)}) %all-to-all-start) | async-done | bytes 4325408 | tf_op jit(solution)/shard_map/all_to_all | solution.py:10
  187.1 8.5 %all-to-all-start.2 = ((bf16[1152,8,256]{2,0,1:T(8,128)(2,1)}), bf16[1152,8,256]{2,0,1:T(8,128)(2,1)}, u32[]{:S(2)}, u32[]{:S(2)}) async-start(bf16[1152,8,256]{2,0,1:T(8,128)(2,1)} %copy.54), calls=%async_computation.3 | async-start | bytes 9437184 | tf_op jit(solution)/shard_map/all_to_all | solution.py:33
  195.6 0.2 fusion.46
  195.9 2.1 fusion.32
  198.0 2.7 fusion.35
  200.7 2.7 fusion.38
  203.3 2.1 fusion.19
  205.4 2.6 fusion.3
  208.0 42.0 %all-to-all-done.2 = bf16[1152,8,256]{2,0,1:T(8,128)(2,1)} async-done(((bf16[1152,8,256]{2,0,1:T(8,128)(2,1)}), bf16[1152,8,256]{2,0,1:T(8,128)(2,1)}, u32[]{:S(2)}, u32[]{:S(2)}) %all-to-all-start.2) | async-done | bytes 4718624 | tf_op jit(solution)/shard_map/all_to_all | solution.py:33
  250.0 3.7 %slice_reduce_fusion.1 = (bf16[576,256]{1,0:T(8,128)(2,1)S(1)}, bf16[576,256]{1,0:T(8,128)(2,1)S(1)}) fusion(bf16[1152,8,256]{2,0,1:T(8,128)(2,1)} %all-to-all-done.2), kind=kLoop, calls=%fused_computation.14 | loop fusion | flops 2064384 | bytes 5308416 | tf_op jit(solution)/shard_map/reduce_sum | solution.py:174
  253.7 0.1 convert_element_type.112
  253.8 0.1 convert_element_type.113
  254.0 1.1 pad_maximum_fusion.3
  255.1 38.9 %all-to-all-start.3 = ((bf16[64,18,256]{2,1,0:T(8,128)(2,1)}), bf16[64,18,256]{2,1,0:T(8,128)(2,1)S(1)}, u32[]{:S(2)}, u32[]{:S(2)}) async-start(bf16[64,18,256]{2,1,0:T(8,128)(2,1)} %pad_maximum_fusion.3), calls=%async_computation.4 | async-start | bytes 1572864 | tf_op jit(solution)/shard_map/all_to_all | solution.py:33
  294.1 2.8 multiply_convert_fusion
  296.9 1.1 pad_maximum_fusion.1
  298.0 0.2 mul.184
  298.3 0.3 fusion.80
  298.6 16.9 %all-to-all-done.3 = bf16[64,18,256]{2,1,0:T(8,128)(2,1)S(1)} async-done(((bf16[64,18,256]{2,1,0:T(8,128)(2,1)}), bf16[64,18,256]{2,1,0:T(8,128)(2,1)S(1)}, u32[]{:S(2)}, u32[]{:S(2)}) %all-to-all-start.3) | async-done | bytes 589856 | tf_op jit(solution)/shard_map/all_to_all | solution.py:33
  315.5 1.3 slice_convert_fusion.1
  316.8 1.3 reshape.191
  318.2 1.6 gather_fusion.3
  319.8 1.6 gather_fusion.2
  321.4 1.0 multiply_reduce_fusion.1
  322.4 0.6 broadcast_in_dim.23
  323.0 6.9 %all-to-all-start.4 = ((f32[8,1,640]{2,1,0:T(1,128)}), f32[8,1,640]{2,1,0:T(1,128)S(1)}, u32[]{:S(2)}, u32[]{:S(2)}) async-start(f32[8,1,640]{2,1,0:T(1,128)} %broadcast_in_dim.23), calls=%async_computation.5 | async-start | bytes 40960 | tf_op jit(solution)/shard_map/all_to_all | solution.py:51
  330.0 1.2 reshape.184
  331.2 0.1 reshape.187
  331.4 3.3 all-to-all-done.4
  334.9 0.1 multiply_reduce_fusion.4
  335.2 0.7 multiply_reduce_fusion.2
  335.9 1.5 add_convert_fusion
  337.4 1.7 fusion.42
  (66 shorter events, 1.7 us)
Async XLA Ops:
  7.2 96.6 %copy-start = (bf16[1,176,2048]{2,1,0:T(8,128)(2,1)S(1)}, bf16[1,176,2048]{2,1,0:T(8,128)(2,1)}, u32[]{:S(2)}) copy-start(bf16[1,176,2048]{2,1,0:T(8,128)(2,1)} %param.27) | copy-start | bytes 2162692
  7.2 93.9 %all-gather.2.cloned.1.call-start = ((), (), s32[]{:S(2)}) async-start(), calls=%async_computation.7 | async-start | bytes 5308416 | tf_op jit(solution)/shard_map/all_gather | solution.py:46
  59.3 1.3 copy-start.4
  59.3 1.3 copy-start.5
  59.3 1.3 copy-start.6
  63.2 37.9 %copy-start.11 = (bf16[1,2048,176]{1,2,0:T(8,128)(2,1)S(1)}, bf16[1,2048,176]{1,2,0:T(8,128)(2,1)}, u32[]{:S(2)}) copy-start(bf16[1,2048,176]{1,2,0:T(8,128)(2,1)} %param.26) | copy-start | bytes 2162692
  63.2 123.8 %all-to-all-start = ((bf16[64,32,1056]{2,1,0:T(8,128)(2,1)}), bf16[64,32,1056]{2,1,0:T(8,128)(2,1)}, u32[]{:S(2)}, u32[]{:S(2)}) async-start(bf16[64,32,1056]{2,1,0:T(8,128)(2,1)} %stack.2), calls=%async_computation | async-start | bytes 9437184 | tf_op jit(solution)/shard_map/all_to_all | solution.py:10
  101.1 3.0 copy-start.10
  104.2 1.1 copy-start.13
  111.4 4.4 %copy-start.12 = (bf16[1,2048,176]{1,2,0:T(8,128)(2,1)S(1)}, bf16[1,2048,176]{1,2,0:T(8,128)(2,1)}, u32[]{:S(2)}) copy-start(bf16[1,2048,176]{1,2,0:T(8,128)(2,1)} %param.26) | copy-start | bytes 2162692
  135.8 59.8 %copy-start.9 = (bf16[2048]{0:T(1024)(128)(2,1)S(1)}, bf16[2048]{0:T(1024)(128)(2,1)}, u32[]{:S(2)}) copy-start(bf16[2048]{0:T(1024)(128)(2,1)} %param.21) | copy-start | bytes 12292
  135.8 59.9 %copy-start.2 = (bf16[128,2048]{1,0:T(8,128)(2,1)S(1)}, bf16[128,2048]{1,0:T(8,128)(2,1)}, u32[]{:S(2)}) copy-start(bf16[128,2048]{1,0:T(8,128)(2,1)} %param.16) | copy-start | bytes 1572868
  187.1 63.0 %all-to-all-start.2 = ((bf16[1152,8,256]{2,0,1:T(8,128)(2,1)}), bf16[1152,8,256]{2,0,1:T(8,128)(2,1)}, u32[]{:S(2)}, u32[]{:S(2)}) async-start(bf16[1152,8,256]{2,0,1:T(8,128)(2,1)} %copy.54), calls=%async_computation.3 | async-start | bytes 9437184 | tf_op jit(solution)/shard_map/all_to_all | solution.py:33
  195.9 4.8 %copy-start.8 = (bf16[128,2048]{1,0:T(8,128)(2,1)S(1)}, bf16[128,2048]{1,0:T(8,128)(2,1)}, u32[]{:S(2)}) copy-start(bf16[128,2048]{1,0:T(8,128)(2,1)} %param.17) | copy-start | bytes 1572868
  255.1 60.4 %all-to-all-start.3 = ((bf16[64,18,256]{2,1,0:T(8,128)(2,1)}), bf16[64,18,256]{2,1,0:T(8,128)(2,1)S(1)}, u32[]{:S(2)}, u32[]{:S(2)}) async-start(bf16[64,18,256]{2,1,0:T(8,128)(2,1)} %pad_maximum_fusion.3), calls=%async_computation.4 | async-start | bytes 1572864 | tf_op jit(solution)/shard_map/all_to_all | solution.py:33
  294.0 41.9 %reduce-scatter.2.cloned.1.call-start = ((), (), s32[]{:S(2)}) async-start(), calls=%async_computation.6 | async-start | bytes 1179648 | tf_op jit(solution)/shard_map/reduce_scatter | solution.py:74
  296.9 1.4 copy-start.3
  321.4 13.5 %copy-start.7 = (s32[128,4]{0,1:T(4,128)S(1)}, s32[128,4]{0,1:T(4,128)}, u32[]{:S(2)}) copy-start(s32[128,4]{0,1:T(4,128)} %param.18) | copy-start | bytes 6148
  321.4 17.7 %copy-start.1 = (bf16[1,176,2048]{2,1,0:T(8,128)(2,1)S(1)}, bf16[1,176,2048]{2,1,0:T(8,128)(2,1)}, u32[]{:S(2)}) copy-start(bf16[1,176,2048]{2,1,0:T(8,128)(2,1)} %param.27) | copy-start | bytes 2162692
  323.0 11.6 %all-to-all-start.4 = ((f32[8,1,640]{2,1,0:T(1,128)}), f32[8,1,640]{2,1,0:T(1,128)S(1)}, u32[]{:S(2)}, u32[]{:S(2)}) async-start(f32[8,1,640]{2,1,0:T(1,128)} %broadcast_in_dim.23), calls=%async_computation.5 | async-start | bytes 40960 | tf_op jit(solution)/shard_map/all_to_all | solution.py:51
Sparse Core Ops, SparseCore 0:
  60.7 40.3 all-gather.1
  298.1 35.6 reduce-scatter.1
